TPU v7x, 256 devices: a whole 4x4x8 slice. The times are simulated.
256 devices in a mesh: trial: 4 (over z_lo), south: 4 (over y_lo, core), east: 4 (over x), down: 4 (over z_hi, y_hi).
Axes of the slice: x: 4, y: 4 (y_hi: 2, y_lo: 2; y = y_hi * 2 + y_lo), z: 8 (z_hi: 2, z_lo: 4; z = z_hi * 4 + z_lo), core: 2. Of those that a mesh axis runs over, the one named last changes fastest.
Arguments:
- tracer: float32 [64, 64, 512, 128], P(('trial', 'south'), 'east', 'down'), parts along dimension 0, may hold values from 0.5 to 2
- mobility: float32 [64, 64, 512, 128], P(('trial', 'south'), 'east', 'down'), parts along dimension 0, may hold values from 0.03 to 0.15
- source: float32 [64, 64, 512, 128], P(('trial', 'south'), 'east', 'down'), parts along dimension 0, may hold values from -0.2 to 0.2
Outputs:
- standardized: float32 [64, 64, 512, 128], P(('trial', 'south'), 'east', 'down'), parts along dimension 0
- tracer_end: float32 [64, 64, 512, 128], P(('trial', 'south'), 'east', 'down'), parts along dimension 0
There are 4 independent parts, one for each index of `trial`. A program takes and returns all parts, laid end to end along the dimension named above; each array names one. Nothing has to cross between parts.
All inputs are finite; a program needn't handle non-finite values.
Results may differ from a plain program's by a relative error of at most 0.00002.
Values sent between devices are 32-bit elements; how exact they have to be, the bound alone decides.
A program may use at most 128 MiB of HBM per device.

v0:
```python
import jax
import jax.numpy as jnp
from jax import lax
from jax.sharding import PartitionSpec as P

STEPS = 3


def with_halo(value, sides, width):
    edges = {}
    for axis, dim in sides:
        peers, length = (lax.axis_size(axis), value.shape[dim])
        up = [(i, (i + 1) % peers) for i in range(peers)]
        last = lax.slice_in_dim(value, length - width, length, axis=dim)
        leading = lax.slice_in_dim(value, 0, width, axis=dim)
        edges[dim] = (
            lax.ppermute(last, axis, up),
            lax.ppermute(leading, axis, [(b, a) for a, b in up]),
        )
    done = []
    for _, dim in sides:
        low, high = edges[dim]
        around = [(width, width) if d in done else (0, 0) for d in range(value.ndim)]
        value = jnp.concatenate([jnp.pad(low, around), value, jnp.pad(high, around)], axis=dim)
        done.append(dim)
    return value


def copy_for_each(value, axis):
    copies = jnp.broadcast_to(value, (lax.axis_size(axis), *value.shape))
    return lax.all_to_all(copies, axis, split_axis=0, concat_axis=0, tiled=True)


def taken_together(value, axis):
    everything = copy_for_each(value, axis)
    return jnp.sum(everything, axis=0)


def packed_total(arrays, axis):
    ends = [0]
    for a in arrays:
        ends.append(ends[-1] + a.size)
    total = taken_together(jnp.concatenate([a.ravel() for a in arrays]), axis)
    return tuple((total[b:e].reshape(a.shape) for a, b, e in zip(arrays, ends, ends[1:])))


def strip_edges(values, dims):
    for dim in dims:
        values = lax.slice_in_dim(values, 1, values.shape[dim] - 1, axis=dim)
    return values


def neighbour(values, dim, start, dims):
    others = [other for other in dims if other != dim]
    values = strip_edges(values, others)
    return lax.slice_in_dim(values, start, start + values.shape[dim] - 2, axis=dim)


def one_step(padded, mobility, source):
    middle = strip_edges(padded, (0, 1, 2))
    lower = [neighbour(padded, dim, 0, (0, 1, 2)) for dim in (0, 1, 2)]
    upper = [neighbour(padded, dim, 2, (0, 1, 2)) for dim in (0, 1, 2)]
    spread = lower[0] + upper[0] + lower[1] + upper[1] + lower[2] + upper[2] - 6.0 * middle
    return middle + mobility * spread + source


def body(tracer, mobility, source):
    for step in range(STEPS):
        padded = with_halo(tracer, (("south", 0), ("east", 1), ("down", 2)), 1)
        tracer = one_step(padded, mobility, source)
    count = tracer.shape[2] * lax.axis_size("down")
    guess = 1.0
    moved = tracer - guess
    totals, squares = packed_total(
        (jnp.sum(moved, axis=2, keepdims=True), jnp.sum(moved * moved, axis=2, keepdims=True)),
        "down",
    )
    line_mean = guess + totals / count
    centred = tracer - line_mean
    line_variance = squares / count - totals / count * (totals / count)
    standardized = centred * lax.rsqrt(line_variance + 0.0001)
    return (standardized, tracer)


def solution(mesh):
    in_specs = (
        P(("trial", "south"), "east", "down", None),
        P(("trial", "south"), "east", "down", None),
        P(("trial", "south"), "east", "down", None),
    )
    out_specs = (
        P(("trial", "south"), "east", "down", None),
        P(("trial", "south"), "east", "down", None),
    )
    return jax.shard_map(body, mesh=mesh, in_specs=in_specs, out_specs=out_specs, check_vma=False)
```

profile of v0, /device:TPU:44, one launch (start us, length us, event | category | flops | bytes accessed | tf_op | source)
XLA Modules:
  0.0 152.9 jit_solution(15135447036923437315)
XLA Ops:
  0.6 0.0 copy-start.3
  0.6 1.8 %fusion.46 = (f32[1,16,128,128]{3,2,1,0:T(8,128)S(1)}, f32[1,16,128,128]{3,2,1,0:T(8,128)S(1)}) fusion(f32[4,16,128,128]{3,2,1,0:T(8,128)} %param.3), kind=kLoop, calls=%fused_computation.102 | loop fusion | bytes 4194304 | tf_op jit(solution)/shard_map/slice | solution.py:15
  2.5 0.1 collective-permute-start
  2.6 1.7 %collective-permute-start.1 = (f32[1,16,128,128]{3,2,1,0:T(8,128)S(1)}, f32[1,16,128,128]{3,2,1,0:T(8,128)S(1)}, u32[]{:S(2)}, u32[]{:S(2)}) collective-permute-start(f32[1,16,128,128]{3,2,1,0:T(8,128)S(1)} %get-tuple-element.21), channel_id=1, source_target_pairs={{16,0},{32,16},{48,32},{0,48},{17,1},{33,17},{49,33},{1,49},{18,2}... | collective-permute-start | bytes 3145736 | tf_op jit(solution)/shard_map/ppermute | solution.py:18
  4.3 0.0 copy-done.3
  4.4 1.3 collective-permute-start.2
  5.6 0.8 collective-permute-start.3
  6.5 2.4 %collective-permute-start.4 = (f32[4,16,1,128]{3,2,1,0:T(1,128)S(1)}, f32[4,16,1,128]{3,2,1,0:T(1,128)S(1)}, u32[]{:S(2)}, u32[]{:S(2)}) collective-permute-start(f32[4,16,1,128]{3,2,1,0:T(1,128)S(1)} %get-tuple-element.17), channel_id=1, source_target_pairs={{0,1},{1,2},{2,3},{3,0},{4,5},{5,6},{6,7},{7,4},{8,9},{9,10},{10,1... | collective-permute-start | bytes 98312 | tf_op jit(solution)/shard_map/ppermute | solution.py:17
  8.9 2.7 %collective-permute-done.2 = f32[4,1,128,128]{3,2,1,0:T(8,128)S(1)} collective-permute-done((f32[4,1,128,128]{3,2,1,0:T(8,128)S(1)}, f32[4,1,128,128]{3,2,1,0:T(8,128)S(1)}, u32[]{:S(2)}, u32[]{:S(2)}) %collective-permute-start.2) | collective-permute-done | bytes 262176 | tf_op jit(solution)/shard_map/ppermute | solution.py:17
  11.6 8.2 %collective-permute-start.5 = (f32[4,16,1,128]{3,2,1,0:T(1,128)S(1)}, f32[4,16,1,128]{3,2,1,0:T(1,128)S(1)}, u32[]{:S(2)}, u32[]{:S(2)}) collective-permute-start(f32[4,16,1,128]{3,2,1,0:T(1,128)S(1)} %get-tuple-element.18), channel_id=1, source_target_pairs={{1,0},{2,1},{3,2},{0,3},{5,4},{6,5},{7,6},{4,7},{9,8},{10,9},{11,1... | collective-permute-start | bytes 98312 | tf_op jit(solution)/shard_map/ppermute | solution.py:18
  19.8 0.0 collective-permute-done.3
  19.9 8.1 %collective-permute-done = f32[1,16,128,128]{3,2,1,0:T(8,128)S(1)} collective-permute-done((f32[1,16,128,128]{3,2,1,0:T(8,128)S(1)}, f32[1,16,128,128]{3,2,1,0:T(8,128)S(1)}, u32[]{:S(2)}, u32[]{:S(2)}) %collective-permute-start) | collective-permute-done | bytes 1048608 | tf_op jit(solution)/shard_map/ppermute | solution.py:17
  28.0 1.1 constant_dynamic-update-slice_fusion.2
  29.0 0.0 copy-start
  29.0 0.0 copy-start.1
  29.0 2.4 %constant_dynamic-update-slice_fusion.1 = f32[6,16,128,128]{3,2,1,0:T(8,128)} fusion(f32[6,16,128,128]{3,2,1,0:T(8,128)} %constant_dynamic-update-slice_fusion.2, f32[4,16,128,128]{3,2,1,0:T(8,128)S(1)} %copy-done.3), kind=kLoop, calls=%fused_computation.92 | loop fusion | bytes 8388608
  31.5 0.0 collective-permute-done.1
  31.5 1.1 constant_dynamic-update-slice_fusion
  32.5 0.0 collective-permute-done.4
  32.5 0.0 collective-permute-done.5
  32.5 0.6 copy-done
  33.1 1.3 copy-done.1
  34.4 13.9 %fusion.27 = f32[4,16,128,128]{3,2,1,0:T(8,128)} fusion(f32[4,16,128,128]{3,2,1,0:T(8,128)S(1)} %copy-done, f32[4,16,128,128]{3,2,1,0:T(8,128)} %param.3, f32[4,16,128,128]{3,2,1,0:T(8,128)S(1)} %copy-done.1, f32[4,16,1,128]{3,2,1,0:T(1,128)S(1)} %collective-permute-done.5, f32[6,1,128,128]{3,2,1,0:T(8,128)S(1)} %pad.39, ...), kind=kLoop, calls=%fused_computation.64 | loop fusion | flops 27262976 | bytes 26017792 | tf_op jit(solution)/shard_map/add | solution.py:64
  48.3 0.0 copy-start.2
  48.3 1.8 %fusion.42 = (f32[1,16,128,128]{3,2,1,0:T(8,128)S(1)}, f32[1,16,128,128]{3,2,1,0:T(8,128)S(1)}) fusion(f32[4,16,128,128]{3,2,1,0:T(8,128)} %fusion.27), kind=kLoop, calls=%fused_computation.98 | loop fusion | bytes 4194304 | tf_op jit(solution)/shard_map/slice | solution.py:14
  50.2 0.1 collective-permute-start.6
  50.3 1.7 %collective-permute-start.7 = (f32[1,16,128,128]{3,2,1,0:T(8,128)S(1)}, f32[1,16,128,128]{3,2,1,0:T(8,128)S(1)}, u32[]{:S(2)}, u32[]{:S(2)}) collective-permute-start(f32[1,16,128,128]{3,2,1,0:T(8,128)S(1)} %get-tuple-element.14), channel_id=1, source_target_pairs={{16,0},{32,16},{48,32},{0,48},{17,1},{33,17},{49,33},{1,49},{18,2}... | collective-permute-start | bytes 3145736 | tf_op jit(solution)/shard_map/ppermute | solution.py:18
  52.0 0.0 copy-done.2
  52.0 1.3 collective-permute-start.8
  53.3 0.8 collective-permute-start.9
  54.2 2.3 %collective-permute-start.10 = (f32[4,16,1,128]{3,2,1,0:T(1,128)S(1)}, f32[4,16,1,128]{3,2,1,0:T(1,128)S(1)}, u32[]{:S(2)}, u32[]{:S(2)}) collective-permute-start(f32[4,16,1,128]{3,2,1,0:T(1,128)S(1)} %get-tuple-element.11), channel_id=1, source_target_pairs={{0,1},{1,2},{2,3},{3,0},{4,5},{5,6},{6,7},{7,4},{8,9},{9,10},{10,1... | collective-permute-start | bytes 98312 | tf_op jit(solution)/shard_map/ppermute | solution.py:17
  56.5 2.7 %collective-permute-done.8 = f32[4,1,128,128]{3,2,1,0:T(8,128)S(1)} collective-permute-done((f32[4,1,128,128]{3,2,1,0:T(8,128)S(1)}, f32[4,1,128,128]{3,2,1,0:T(8,128)S(1)}, u32[]{:S(2)}, u32[]{:S(2)}) %collective-permute-start.8) | collective-permute-done | bytes 262176 | tf_op jit(solution)/shard_map/ppermute | solution.py:17
  59.2 7.7 %collective-permute-start.11 = (f32[4,16,1,128]{3,2,1,0:T(1,128)S(1)}, f32[4,16,1,128]{3,2,1,0:T(1,128)S(1)}, u32[]{:S(2)}, u32[]{:S(2)}) collective-permute-start(f32[4,16,1,128]{3,2,1,0:T(1,128)S(1)} %get-tuple-element.12), channel_id=1, source_target_pairs={{1,0},{2,1},{3,2},{0,3},{5,4},{6,5},{7,6},{4,7},{9,8},{10,9},{11,1... | collective-permute-start | bytes 98312 | tf_op jit(solution)/shard_map/ppermute | solution.py:18
  66.9 0.0 collective-permute-done.9
  67.0 7.0 %collective-permute-done.10 = f32[4,16,1,128]{3,2,1,0:T(1,128)S(1)} collective-permute-done((f32[4,16,1,128]{3,2,1,0:T(1,128)S(1)}, f32[4,16,1,128]{3,2,1,0:T(1,128)S(1)}, u32[]{:S(2)}, u32[]{:S(2)}) %collective-permute-start.10) | collective-permute-done | bytes 32800 | tf_op jit(solution)/shard_map/ppermute | solution.py:17
  74.0 3.3 %collective-permute-done.11 = f32[4,16,1,128]{3,2,1,0:T(1,128)S(1)} collective-permute-done((f32[4,16,1,128]{3,2,1,0:T(1,128)S(1)}, f32[4,16,1,128]{3,2,1,0:T(1,128)S(1)}, u32[]{:S(2)}, u32[]{:S(2)}) %collective-permute-start.11) | collective-permute-done | bytes 32800 | tf_op jit(solution)/shard_map/ppermute | solution.py:18
  77.3 0.0 collective-permute-done.6
  77.3 0.0 collective-permute-done.7
  77.3 7.6 %fusion.16 = f32[4,16,128,128]{3,2,1,0:T(8,128)S(1)} fusion(f32[4,16,128,128]{3,2,1,0:T(8,128)S(1)} %copy-done, f32[4,16,128,128]{3,2,1,0:T(8,128)S(1)} %copy-done.2, f32[4,16,128,128]{3,2,1,0:T(8,128)S(1)} %copy-done.1, f32[4,16,1,128]{3,2,1,0:T(1,128)S(1)} %collective-permute-done.11, f32[6,1,128,128]{3,2,1,0:T(8,128)S(1)} %pad.43, ...), kind=kLoop, calls=%fused_computation.35 | loop fusion | flops 35651584 | bytes 19726336 | tf_op jit(solution)/shard_map/add | solution.py:64
  85.0 0.2 fusion.40
  85.2 0.1 collective-permute-start.12
  85.3 1.7 %collective-permute-start.13 = (f32[1,16,128,128]{3,2,1,0:T(8,128)S(1)}, f32[1,16,128,128]{3,2,1,0:T(8,128)S(1)}, u32[]{:S(2)}, u32[]{:S(2)}) collective-permute-start(f32[1,16,128,128]{3,2,1,0:T(8,128)S(1)} %get-tuple-element.10), channel_id=1, source_target_pairs={{16,0},{32,16},{48,32},{0,48},{17,1},{33,17},{49,33},{1,49},{18,2}... | collective-permute-start | bytes 3145736 | tf_op jit(solution)/shard_map/ppermute | solution.py:18
  87.0 1.3 collective-permute-start.14
  88.3 0.8 collective-permute-start.15
  89.2 0.8 collective-permute-start.16
  90.0 6.2 %collective-permute-done.14 = f32[4,1,128,128]{3,2,1,0:T(8,128)S(1)} collective-permute-done((f32[4,1,128,128]{3,2,1,0:T(8,128)S(1)}, f32[4,1,128,128]{3,2,1,0:T(8,128)S(1)}, u32[]{:S(2)}, u32[]{:S(2)}) %collective-permute-start.14) | collective-permute-done | bytes 262176 | tf_op jit(solution)/shard_map/ppermute | solution.py:17
  96.1 5.3 %collective-permute-start.17 = (f32[4,16,1,128]{3,2,1,0:T(1,128)S(1)}, f32[4,16,1,128]{3,2,1,0:T(1,128)S(1)}, u32[]{:S(2)}, u32[]{:S(2)}) collective-permute-start(f32[4,16,1,128]{3,2,1,0:T(1,128)S(1)} %get-tuple-element.6), channel_id=1, source_target_pairs={{1,0},{2,1},{3,2},{0,3},{5,4},{6,5},{7,6},{4,7},{9,8},{10,9},{11,1... | collective-permute-start | bytes 98312 | tf_op jit(solution)/shard_map/ppermute | solution.py:18
  101.5 0.0 collective-permute-done.15
  101.5 10.3 %collective-permute-done.16 = f32[4,16,1,128]{3,2,1,0:T(1,128)S(1)} collective-permute-done((f32[4,16,1,128]{3,2,1,0:T(1,128)S(1)}, f32[4,16,1,128]{3,2,1,0:T(1,128)S(1)}, u32[]{:S(2)}, u32[]{:S(2)}) %collective-permute-start.16) | collective-permute-done | bytes 32800 | tf_op jit(solution)/shard_map/ppermute | solution.py:17
  111.8 0.3 collective-permute-done.17
  112.1 0.0 collective-permute-done.12
  112.1 0.0 collective-permute-done.13
  112.1 10.4 %add_reduce_fusion = (f32[4,16,128]{2,1,0:T(8,128)S(1)}, f32[4,16,128]{2,1,0:T(8,128)S(1)}, f32[4,16,128,128]{3,2,1,0:T(8,128)}) fusion(f32[4,16,128,128]{3,2,1,0:T(8,128)S(1)} %copy-done, f32[4,16,128,128]{3,2,1,0:T(8,128)S(1)} %fusion.16, f32[4,16,128,128]{3,2,1,0:T(8,128)S(1)} %copy-done.1, f32[4,16,1,128]{3,2,1,0:T(1,128)S(1)} %collective-permute-done.17, ...), kind=kLoop, calls=%fused_computation.83 | loop fusion | flops 39829504 | bytes 19791872 | tf_op jit(solution)/shard_map/reduce_sum | solution.py:75
  122.5 0.1 broadcast_in_dim.3
  122.6 24.8 %all_to_all.6 = f32[4,1,16384]{2,1,0:T(1,128)S(1)} all-to-all(f32[4,1,16384]{2,1,0:T(1,128)S(1)} %broadcast_in_dim.3), channel_id=1, replica_groups=mesh['trial'=4,'south'=4,'east'=4,'down'=4] {'down'}, dimensions={0} | all-to-all | bytes 524288 | tf_op jit(solution)/shard_map/all_to_all | solution.py:31
  147.4 0.2 reduce_sum.29
  147.6 5.2 %subtract_multiply_fusion = f32[4,16,128,128]{3,2,1,0:T(8,128)} fusion(f32[4,16,128,128]{3,2,1,0:T(8,128)} %get-tuple-element.4, f32[4,16,128]{2,1,0:T(8,128)S(1)} %bitcast.7, f32[4,16,128]{2,1,0:T(8,128)S(1)} %bitcast.6), kind=kLoop, calls=%fused_computation.81 | loop fusion | flops 2097152 | bytes 8454144 | tf_op jit(solution)/shard_map/mul | solution.py:81
  (14 shorter events, 0.4 us)
Async XLA Ops:
  0.6 3.7 %copy-start.3 = (f32[4,16,128,128]{3,2,1,0:T(8,128)S(1)}, f32[4,16,128,128]{3,2,1,0:T(8,128)}, u32[]{:S(2)}) copy-start(f32[4,16,128,128]{3,2,1,0:T(8,128)} %param.3) | copy-start | bytes 12582916
  2.5 25.5 %collective-permute-start = (f32[1,16,128,128]{3,2,1,0:T(8,128)S(1)}, f32[1,16,128,128]{3,2,1,0:T(8,128)S(1)}, u32[]{:S(2)}, u32[]{:S(2)}) collective-permute-start(f32[1,16,128,128]{3,2,1,0:T(8,128)S(1)} %get-tuple-element.22), channel_id=1, source_target_pairs={{0,16},{16,32},{32,48},{48,0},{1,17},{17,33},{33,49},{49,1},{2,18}... | collective-permute-start | bytes 3145736 | tf_op jit(solution)/shard_map/ppermute | solution.py:17
  2.6 28.9 %collective-permute-start.1 = (f32[1,16,128,128]{3,2,1,0:T(8,128)S(1)}, f32[1,16,128,128]{3,2,1,0:T(8,128)S(1)}, u32[]{:S(2)}, u32[]{:S(2)}) collective-permute-start(f32[1,16,128,128]{3,2,1,0:T(8,128)S(1)} %get-tuple-element.21), channel_id=1, source_target_pairs={{16,0},{32,16},{48,32},{0,48},{17,1},{33,17},{49,33},{1,49},{18,2}... | collective-permute-start | bytes 3145736 | tf_op jit(solution)/shard_map/ppermute | solution.py:18
  4.4 7.3 %collective-permute-start.2 = (f32[4,1,128,128]{3,2,1,0:T(8,128)S(1)}, f32[4,1,128,128]{3,2,1,0:T(8,128)S(1)}, u32[]{:S(2)}, u32[]{:S(2)}) collective-permute-start(f32[4,1,128,128]{3,2,1,0:T(8,128)S(1)} %get-tuple-element.19), channel_id=1, source_target_pairs={{0,4},{4,8},{8,12},{12,0},{1,5},{5,9},{9,13},{13,1},{2,6},{6,10},{... | collective-permute-start | bytes 786440 | tf_op jit(solution)/shard_map/ppermute | solution.py:17
  5.6 14.2 %collective-permute-start.3 = (f32[4,1,128,128]{3,2,1,0:T(8,128)S(1)}, f32[4,1,128,128]{3,2,1,0:T(8,128)S(1)}, u32[]{:S(2)}, u32[]{:S(2)}) collective-permute-start(f32[4,1,128,128]{3,2,1,0:T(8,128)S(1)} %get-tuple-element.20), channel_id=1, source_target_pairs={{4,0},{8,4},{12,8},{0,12},{5,1},{9,5},{13,9},{1,13},{6,2},{10,6},{... | collective-permute-start | bytes 786440 | tf_op jit(solution)/shard_map/ppermute | solution.py:18
  6.5 26.0 %collective-permute-start.4 = (f32[4,16,1,128]{3,2,1,0:T(1,128)S(1)}, f32[4,16,1,128]{3,2,1,0:T(1,128)S(1)}, u32[]{:S(2)}, u32[]{:S(2)}) collective-permute-start(f32[4,16,1,128]{3,2,1,0:T(1,128)S(1)} %get-tuple-element.17), channel_id=1, source_target_pairs={{0,1},{1,2},{2,3},{3,0},{4,5},{5,6},{6,7},{7,4},{8,9},{9,10},{10,1... | collective-permute-start | bytes 98312 | tf_op jit(solution)/shard_map/ppermute | solution.py:17
  11.6 20.9 %collective-permute-start.5 = (f32[4,16,1,128]{3,2,1,0:T(1,128)S(1)}, f32[4,16,1,128]{3,2,1,0:T(1,128)S(1)}, u32[]{:S(2)}, u32[]{:S(2)}) collective-permute-start(f32[4,16,1,128]{3,2,1,0:T(1,128)S(1)} %get-tuple-element.18), channel_id=1, source_target_pairs={{1,0},{2,1},{3,2},{0,3},{5,4},{6,5},{7,6},{4,7},{9,8},{10,9},{11,1... | collective-permute-start | bytes 98312 | tf_op jit(solution)/shard_map/ppermute | solution.py:18
  29.0 4.1 %copy-start = (f32[4,16,128,128]{3,2,1,0:T(8,128)S(1)}, f32[4,16,128,128]{3,2,1,0:T(8,128)}, u32[]{:S(2)}) copy-start(f32[4,16,128,128]{3,2,1,0:T(8,128)} %param.5) | copy-start | bytes 12582916
  29.0 5.4 %copy-start.1 = (f32[4,16,128,128]{3,2,1,0:T(8,128)S(1)}, f32[4,16,128,128]{3,2,1,0:T(8,128)}, u32[]{:S(2)}) copy-start(f32[4,16,128,128]{3,2,1,0:T(8,128)} %param.4) | copy-start | bytes 12582916
  48.3 3.7 %copy-start.2 = (f32[4,16,128,128]{3,2,1,0:T(8,128)S(1)}, f32[4,16,128,128]{3,2,1,0:T(8,128)}, u32[]{:S(2)}) copy-start(f32[4,16,128,128]{3,2,1,0:T(8,128)} %fusion.27) | copy-start | bytes 12582916
  50.2 27.1 %collective-permute-start.6 = (f32[1,16,128,128]{3,2,1,0:T(8,128)S(1)}, f32[1,16,128,128]{3,2,1,0:T(8,128)S(1)}, u32[]{:S(2)}, u32[]{:S(2)}) collective-permute-start(f32[1,16,128,128]{3,2,1,0:T(8,128)S(1)} %get-tuple-element.13), channel_id=1, source_target_pairs={{0,16},{16,32},{32,48},{48,0},{1,17},{17,33},{33,49},{49,1},{2,18}... | collective-permute-start | bytes 3145736 | tf_op jit(solution)/shard_map/ppermute | solution.py:17
  50.3 27.0 %collective-permute-start.7 = (f32[1,16,128,128]{3,2,1,0:T(8,128)S(1)}, f32[1,16,128,128]{3,2,1,0:T(8,128)S(1)}, u32[]{:S(2)}, u32[]{:S(2)}) collective-permute-start(f32[1,16,128,128]{3,2,1,0:T(8,128)S(1)} %get-tuple-element.14), channel_id=1, source_target_pairs={{16,0},{32,16},{48,32},{0,48},{17,1},{33,17},{49,33},{1,49},{18,2}... | collective-permute-start | bytes 3145736 | tf_op jit(solution)/shard_map/ppermute | solution.py:18
  52.0 7.1 %collective-permute-start.8 = (f32[4,1,128,128]{3,2,1,0:T(8,128)S(1)}, f32[4,1,128,128]{3,2,1,0:T(8,128)S(1)}, u32[]{:S(2)}, u32[]{:S(2)}) collective-permute-start(f32[4,1,128,128]{3,2,1,0:T(8,128)S(1)} %get-tuple-element.15), channel_id=1, source_target_pairs={{0,4},{4,8},{8,12},{12,0},{1,5},{5,9},{9,13},{13,1},{2,6},{6,10},{... | collective-permute-start | bytes 786440 | tf_op jit(solution)/shard_map/ppermute | solution.py:17
  53.3 13.6 %collective-permute-start.9 = (f32[4,1,128,128]{3,2,1,0:T(8,128)S(1)}, f32[4,1,128,128]{3,2,1,0:T(8,128)S(1)}, u32[]{:S(2)}, u32[]{:S(2)}) collective-permute-start(f32[4,1,128,128]{3,2,1,0:T(8,128)S(1)} %get-tuple-element.16), channel_id=1, source_target_pairs={{4,0},{8,4},{12,8},{0,12},{5,1},{9,5},{13,9},{1,13},{6,2},{10,6},{... | collective-permute-start | bytes 786440 | tf_op jit(solution)/shard_map/ppermute | solution.py:18
  54.2 19.8 %collective-permute-start.10 = (f32[4,16,1,128]{3,2,1,0:T(1,128)S(1)}, f32[4,16,1,128]{3,2,1,0:T(1,128)S(1)}, u32[]{:S(2)}, u32[]{:S(2)}) collective-permute-start(f32[4,16,1,128]{3,2,1,0:T(1,128)S(1)} %get-tuple-element.11), channel_id=1, source_target_pairs={{0,1},{1,2},{2,3},{3,0},{4,5},{5,6},{6,7},{7,4},{8,9},{9,10},{10,1... | collective-permute-start | bytes 98312 | tf_op jit(solution)/shard_map/ppermute | solution.py:17
  59.2 18.1 %collective-permute-start.11 = (f32[4,16,1,128]{3,2,1,0:T(1,128)S(1)}, f32[4,16,1,128]{3,2,1,0:T(1,128)S(1)}, u32[]{:S(2)}, u32[]{:S(2)}) collective-permute-start(f32[4,16,1,128]{3,2,1,0:T(1,128)S(1)} %get-tuple-element.12), channel_id=1, source_target_pairs={{1,0},{2,1},{3,2},{0,3},{5,4},{6,5},{7,6},{4,7},{9,8},{10,9},{11,1... | collective-permute-start | bytes 98312 | tf_op jit(solution)/shard_map/ppermute | solution.py:18
  85.2 26.9 %collective-permute-start.12 = (f32[1,16,128,128]{3,2,1,0:T(8,128)S(1)}, f32[1,16,128,128]{3,2,1,0:T(8,128)S(1)}, u32[]{:S(2)}, u32[]{:S(2)}) collective-permute-start(f32[1,16,128,128]{3,2,1,0:T(8,128)S(1)} %get-tuple-element.9), channel_id=1, source_target_pairs={{0,16},{16,32},{32,48},{48,0},{1,17},{17,33},{33,49},{49,1},{2,18}... | collective-permute-start | bytes 3145736 | tf_op jit(solution)/shard_map/ppermute | solution.py:17
  85.3 26.8 %collective-permute-start.13 = (f32[1,16,128,128]{3,2,1,0:T(8,128)S(1)}, f32[1,16,128,128]{3,2,1,0:T(8,128)S(1)}, u32[]{:S(2)}, u32[]{:S(2)}) collective-permute-start(f32[1,16,128,128]{3,2,1,0:T(8,128)S(1)} %get-tuple-element.10), channel_id=1, source_target_pairs={{16,0},{32,16},{48,32},{0,48},{17,1},{33,17},{49,33},{1,49},{18,2}... | collective-permute-start | bytes 3145736 | tf_op jit(solution)/shard_map/ppermute | solution.py:18
  87.0 9.1 %collective-permute-start.14 = (f32[4,1,128,128]{3,2,1,0:T(8,128)S(1)}, f32[4,1,128,128]{3,2,1,0:T(8,128)S(1)}, u32[]{:S(2)}, u32[]{:S(2)}) collective-permute-start(f32[4,1,128,128]{3,2,1,0:T(8,128)S(1)} %get-tuple-element.7), channel_id=1, source_target_pairs={{0,4},{4,8},{8,12},{12,0},{1,5},{5,9},{9,13},{13,1},{2,6},{6,10},{... | collective-permute-start | bytes 786440 | tf_op jit(solution)/shard_map/ppermute | solution.py:17
  88.3 13.2 %collective-permute-start.15 = (f32[4,1,128,128]{3,2,1,0:T(8,128)S(1)}, f32[4,1,128,128]{3,2,1,0:T(8,128)S(1)}, u32[]{:S(2)}, u32[]{:S(2)}) collective-permute-start(f32[4,1,128,128]{3,2,1,0:T(8,128)S(1)} %get-tuple-element.8), channel_id=1, source_target_pairs={{4,0},{8,4},{12,8},{0,12},{5,1},{9,5},{13,9},{1,13},{6,2},{10,6},{... | collective-permute-start | bytes 786440 | tf_op jit(solution)/shard_map/ppermute | solution.py:18
  89.2 22.7 %collective-permute-start.16 = (f32[4,16,1,128]{3,2,1,0:T(1,128)S(1)}, f32[4,16,1,128]{3,2,1,0:T(1,128)S(1)}, u32[]{:S(2)}, u32[]{:S(2)}) collective-permute-start(f32[4,16,1,128]{3,2,1,0:T(1,128)S(1)} %get-tuple-element.5), channel_id=1, source_target_pairs={{0,1},{1,2},{2,3},{3,0},{4,5},{5,6},{6,7},{7,4},{8,9},{9,10},{10,1... | collective-permute-start | bytes 98312 | tf_op jit(solution)/shard_map/ppermute | solution.py:17
  96.1 16.0 %collective-permute-start.17 = (f32[4,16,1,128]{3,2,1,0:T(1,128)S(1)}, f32[4,16,1,128]{3,2,1,0:T(1,128)S(1)}, u32[]{:S(2)}, u32[]{:S(2)}) collective-permute-start(f32[4,16,1,128]{3,2,1,0:T(1,128)S(1)} %get-tuple-element.6), channel_id=1, source_target_pairs={{1,0},{2,1},{3,2},{0,3},{5,4},{6,5},{7,6},{4,7},{9,8},{10,9},{11,1... | collective-permute-start | bytes 98312 | tf_op jit(solution)/shard_map/ppermute | solution.py:18
where the time goes:
time: 153 us
  waiting for transfers between devices  40.7 us (27%)
  starting transfers between devices  38.3 us (25%)
  other arithmetic  37.4 us (24%)
  blocking collectives  24.8 us (16%)
  local copies, waits for them, and re-layouts  10.8 us (7%)
    ppermute x9, waiting for transfers between devices, with_halo(): lax.ppermute(last, axis, up)  37.1 us
    ppermute x9, starting transfers between devices, with_halo(): lax.ppermute(leading, axis, [(b, a) for a, b in up])  28.9 us
    all_to_all x1, blocking collectives, copy_for_each(): return lax.all_to_all(copies, axis, split_axis=0, concat_axis=0, tiled=True)  24.8 us
    add x2, other arithmetic, one_step(): return middle + mobility * spread + source  21.6 us
    reduce_sum x1, other arithmetic, body(): jnp.sum(moved, axis=2, keepdims=True)  10.4 us
    ppermute x9, starting transfers between devices, with_halo(): lax.ppermute(last, axis, up)  9.46 us
    unnamed x10, local copies, waits for them, and re-layouts  5.36 us
    mul x1, other arithmetic, body(): standardized = centred * lax.rsqrt(line_variance + 0.0001)  5.23 us
  transfers between devices with their start and end apart: 18, of which 8 were waited for; matrix products, arithmetic and copies ran while one was open for 3% of the time, Pallas kernels for 0%

commit v1 on v0

v1 whole, which is shorter than its diff:
```python
import functools

import jax
import jax.numpy as jnp
from jax import lax
from jax.experimental import pallas as pl
from jax.experimental.pallas import tpu as pltpu
from jax.sharding import PartitionSpec as P

STEPS = 3
AHEAD = 4
LAG = 3
MESH = pl.DeviceIdType.MESH


def kernel(
    sizes,
    tr, mo, so,
    std_o, tr_o,
    u, m, s, st, zs, zr, ms, mr,
    in_sem, out_sem,
    s_send, s_recv, e_send, e_recv, z_send, z_recv, m_send, m_recv,
):
    souths, easts, downs = sizes
    Y, X, Z, L = tr.shape
    pairs = X // 2
    rows = 2 * Y
    at = {name: lax.axis_index(name) for name in ("south", "east", "down")}

    def peer(name, count, shift):
        return {name: lax.rem(at[name] + shift + count, count)}

    def south(side, t, x):
        return pltpu.make_async_remote_copy(
            src_ref=u.at[t, Y if side else 1, x + 1],
            dst_ref=u.at[t, 0 if side else Y + 1, x + 1],
            send_sem=s_send.at[side, t, x],
            recv_sem=s_recv.at[side, t, x],
            device_id=peer("south", souths, 1 if side else -1),
            device_id_type=MESH,
        )

    def east(side, t):
        return pltpu.make_async_remote_copy(
            src_ref=u.at[t, pl.ds(1, Y), X if side else 1],
            dst_ref=u.at[t, pl.ds(1, Y), 0 if side else X + 1],
            send_sem=e_send.at[side, t],
            recv_sem=e_recv.at[side, t],
            device_id=peer("east", easts, 1 if side else -1),
            device_id_type=MESH,
        )

    def down(side, t, j):
        return pltpu.make_async_remote_copy(
            src_ref=zs.at[t, side, j],
            dst_ref=zr.at[t, side, j],
            send_sem=z_send.at[side, t, j],
            recv_sem=z_recv.at[side, t, j],
            device_id=peer("down", downs, 1 if side else -1),
            device_id_type=MESH,
        )

    def moments(d, j):
        return pltpu.make_async_remote_copy(
            src_ref=ms.at[j],
            dst_ref=mr.at[d - 1, j],
            send_sem=m_send.at[d - 1, j],
            recv_sem=m_recv.at[d - 1, j],
            device_id=peer("down", downs, d),
            device_id_type=MESH,
        )

    def south_pair(t, j):
        for side in (0, 1):
            for x in (j, X - 1 - j):
                south(side, t, x).start()

    def save_line(t, y, x):
        return pltpu.make_async_copy(u.at[t, pl.ds(1, Y), x + 1], tr_o.at[:, x], out_sem.at[0, x])

    def save_std(x):
        return pltpu.make_async_copy(st.at[:, x], std_o.at[:, x], out_sem.at[1, x])

    loads = [
        pltpu.make_async_copy(tr.at[y], u.at[0, y + 1, pl.ds(1, X)], in_sem.at[y])
        for y in range(Y)
    ]
    for y in [0, Y - 1] + list(range(1, Y - 1)):
        loads[y].start()
    others = [
        pltpu.make_async_copy(mo, m, in_sem.at[Y]),
        pltpu.make_async_copy(so, s, in_sem.at[Y + 1]),
    ]
    for copy in others:
        copy.start()

    barrier = pltpu.get_barrier_semaphore()
    greet = [peer("south", souths, d) for d in (-1, 1)]
    greet += [peer("east", easts, d) for d in (-1, 1)]
    greet += [peer("down", downs, d) for d in range(1, downs)]
    for who in greet:
        pl.semaphore_signal(barrier, inc=1, device_id=who, device_id_type=MESH)
    pl.semaphore_wait(barrier, len(greet))

    for copy in loads:
        copy.wait()

    def first_faces(j, carry):
        for r, x in enumerate((j, X - 1 - j)):
            for y in range(Y):
                zs[0, 0, j, pl.ds(r * Y + y, 1), :] = u[0, y + 1, x + 1, pl.ds(0, 1), :]
                zs[0, 1, j, pl.ds(r * Y + y, 1), :] = u[0, y + 1, x + 1, pl.ds(Z - 1, 1), :]
        return carry

    lax.fori_loop(0, pairs, first_faces, 0)
    south_pair(0, 0)
    for side in (0, 1):
        east(side, 0).start()

    def first_down(j, carry):
        for side in (0, 1):
            down(side, 0, j).start()
        return carry

    lax.fori_loop(0, pairs, first_down, 0)
    for j in range(1, AHEAD):
        south_pair(0, j)
    for copy in others:
        copy.wait()

    level = lax.broadcasted_iota(jnp.int32, (Z, L), 0)
    top, bottom = level == 0, level == Z - 1

    def advance(t, j):
        for side in (0, 1):
            down(side, t, j).wait_recv()
            for x in (j, X - 1 - j):
                south(side, t, x).wait_recv()

        @pl.when(j == 0)
        def _():
            for side in (0, 1):
                east(side, t).wait_recv()

        for r, x in enumerate((j, X - 1 - j)):
            for y in range(Y):
                at_row = pl.ds(r * Y + y, 1)
                middle = u[t, y + 1, x + 1]
                before = jnp.where(top, zr[t, 1, j, at_row, :], pltpu.roll(middle, 1, 0))
                after = jnp.where(bottom, zr[t, 0, j, at_row, :], pltpu.roll(middle, Z - 1, 0))
                spread = u[t, y, x + 1] + u[t, y + 2, x + 1] + u[t, y + 1, x] + u[t, y + 1, x + 2]
                spread = spread + before + after - 6.0 * middle
                value = middle + m[y, x] * spread + s[y, x]
                u[t + 1, y + 1, x + 1] = value
                if t + 1 < STEPS:
                    zs[t + 1, 0, j, at_row, :] = value[:1]
                    zs[t + 1, 1, j, at_row, :] = value[Z - 1 :]
                else:
                    mean = jnp.sum(value, axis=0, keepdims=True) * (1.0 / Z)
                    off = value - mean
                    ms[j, 0, at_row, :] = mean
                    ms[j, 1, at_row, :] = jnp.sum(off * off, axis=0, keepdims=True)

    def finish(j):
        for d in range(1, downs):
            moments(d, j).wait_recv()
        means = [ms[j, 0]] + [mr[d, j, 0] for d in range(downs - 1)]
        total = functools.reduce(jnp.add, means)
        spreads = functools.reduce(jnp.add, [ms[j, 1]] + [mr[d, j, 1] for d in range(downs - 1)])
        mean = total * (1.0 / downs)
        between = functools.reduce(jnp.add, [(a - mean) * (a - mean) for a in means])
        variance = (spreads + between * Z) * (1.0 / (Z * downs))
        scale = lax.rsqrt(variance + 0.0001)
        for r, x in enumerate((j, X - 1 - j)):
            for y in range(Y):
                k = r * Y + y
                st[y, x] = (u[STEPS, y + 1, x + 1] - mean[k : k + 1]) * scale[k : k + 1]
        for x in (j, X - 1 - j):
            save_std(x).start()

    for t in range(STEPS):

        def step(j, carry, t=t):
            advance(t, j)
            if t + 1 < STEPS:
                for side in (0, 1):
                    down(side, t + 1, j).start()

                @pl.when(j == 0)
                def _():
                    for side in (0, 1):
                        east(side, t + 1).start()

                n = t * pairs + j + AHEAD
                south_pair(n // pairs, n % pairs)
            else:
                for d in range(1, downs):
                    moments(d, j).start()
                for x in (j, X - 1 - j):
                    save_line(STEPS, 0, x).start()

                @pl.when(j + AHEAD < pairs)
                def _():
                    south_pair(t, j + AHEAD)

                @pl.when(j >= LAG)
                def _():
                    finish(j - LAG)

            return carry

        lax.fori_loop(0, pairs, step, 0)

    def tail(j, carry):
        finish(j)
        return carry

    lax.fori_loop(pairs - LAG, pairs, tail, 0)

    def drain(x, carry):
        save_line(STEPS, 0, x).wait()
        save_std(x).wait()
        for side in (0, 1):
            for t in range(STEPS):
                south(side, t, x).wait_send()
        return carry

    lax.fori_loop(0, X, drain, 0)

    def drain_pairs(j, carry):
        for side in (0, 1):
            for t in range(STEPS):
                down(side, t, j).wait_send()
        for d in range(1, downs):
            moments(d, j).wait_send()
        return carry

    lax.fori_loop(0, pairs, drain_pairs, 0)
    for side in (0, 1):
        for t in range(STEPS):
            east(side, t).wait_send()


def body(tracer, mobility, source):
    sizes = tuple(lax.axis_size(a) for a in ("south", "east", "down"))
    Y, X, Z, L = tracer.shape
    downs, pairs = sizes[2], X // 2
    f32 = jnp.float32
    dma = pltpu.SemaphoreType.DMA
    shape = jax.ShapeDtypeStruct(tracer.shape, f32)
    anywhere = pl.BlockSpec(memory_space=pl.ANY)
    return pl.pallas_call(
        functools.partial(kernel, sizes),
        out_shape=(shape, shape),
        in_specs=[anywhere] * 3,
        out_specs=(anywhere, anywhere),
        scratch_shapes=[
            pltpu.VMEM((STEPS + 1, Y + 2, X + 2, Z, L), f32),
            pltpu.VMEM((Y, X, Z, L), f32),
            pltpu.VMEM((Y, X, Z, L), f32),
            pltpu.VMEM((Y, X, Z, L), f32),
            pltpu.VMEM((STEPS, 2, pairs, 2 * Y, L), f32),
            pltpu.VMEM((STEPS, 2, pairs, 2 * Y, L), f32),
            pltpu.VMEM((pairs, 2, 2 * Y, L), f32),
            pltpu.VMEM((downs - 1, pairs, 2, 2 * Y, L), f32),
            dma((Y + 2,)),
            dma((2, X)),
            dma((2, STEPS, X)),
            dma((2, STEPS, X)),
            dma((2, STEPS)),
            dma((2, STEPS)),
            dma((2, STEPS, pairs)),
            dma((2, STEPS, pairs)),
            dma((downs - 1, pairs)),
            dma((downs - 1, pairs)),
        ],
        compiler_params=pltpu.CompilerParams(
            collective_id=0, has_side_effects=True, vmem_limit_bytes=60 * 1024 * 1024
        ),
    )(tracer, mobility, source)


def solution(mesh):
    spec = P(("trial", "south"), "east", "down", None)
    return jax.shard_map(
        body, mesh=mesh, in_specs=(spec,) * 3, out_specs=(spec,) * 2, check_vma=False
    )
```

time: 153 us -> 103 us (0.67)
  the two profiles are of different devices: /device:TPU:44 before, /device:TPU:1 now
where the time goes in v1:
time: 103 us
  Pallas kernels  95 us (92%)
  local copies, waits for them, and re-layouts  6.87 us (7%)
    pallas_call x1, Pallas kernels, body(): pl.pallas_call(functools.partial(kernel, sizes), out_shape=(shape, shape)...  95 us
    unnamed x4, local copies, waits for them, and re-layouts  6.87 us

profile of v1, /device:TPU:1, one launch (start us, length us, event | category | flops | bytes accessed | tf_op | source)
XLA Modules:
  0.0 102.5 jit_solution(3225408852344272192)
XLA Ops:
  0.6 95.0 %shard_map.50 = (f32[4,16,128,128]{3,2,1,0:T(8,128)}, f32[4,16,128,128]{3,2,1,0:T(8,128)}) custom-call(f32[4,16,128,128]{3,2,1,0:T(8,128)} %tr.1, f32[4,16,128,128]{3,2,1,0:T(8,128)} %mo.1, f32[4,16,128,128]{3,2,1,0:T(8,128)} %so.1), custom_call_target="tpu_custom_call" | custom-call | tf_op jit(solution)/shard_map/pallas_call | solution.py:252
  95.6 0.0 copy-start
  95.6 4.8 %copy.7 = f32[4,16,128,128]{3,2,1,0:T(8,128)} copy(f32[4,16,128,128]{3,2,1,0:T(8,128)} %get-tuple-element.4) | data formatting | bytes 8388608
  100.5 0.0 copy-done
  100.5 2.0 %copy.8 = f32[4,16,128,128]{3,2,1,0:T(8,128)} copy(f32[4,16,128,128]{3,2,1,0:T(8,128)S(1)} %copy-done) | data formatting | bytes 8388608
Async XLA Ops:
  95.6 4.9 %copy-start = (f32[4,16,128,128]{3,2,1,0:T(8,128)S(1)}, f32[4,16,128,128]{3,2,1,0:T(8,128)}, u32[]{:S(2)}) copy-start(f32[4,16,128,128]{3,2,1,0:T(8,128)} %get-tuple-element.5) | copy-start | bytes 12582916

commit v2 on v1

--- a/solution.py
+++ b/solution.py
@@ -16,10 +16,9 @@
 def kernel(
     sizes,
     tr, mo, so,
-    std_o, tr_o,
-    u, m, s, st, zs, zr, ms, mr,
-    in_sem, out_sem,
-    s_send, s_recv, e_send, e_recv, z_send, z_recv, m_send, m_recv,
+    st, end,
+    u, m, s, zs, zr, ms, mr,
+    in_sem, s_send, s_recv, e_send, e_recv, z_send, z_recv, m_send, m_recv,
 ):
     souths, easts, downs = sizes
     Y, X, Z, L = tr.shape
@@ -30,12 +29,12 @@
     def peer(name, count, shift):
         return {name: lax.rem(at[name] + shift + count, count)}
 
-    def south(side, t, x):
+    def south(side, t, j, x):
         return pltpu.make_async_remote_copy(
             src_ref=u.at[t, Y if side else 1, x + 1],
             dst_ref=u.at[t, 0 if side else Y + 1, x + 1],
-            send_sem=s_send.at[side, t, x],
-            recv_sem=s_recv.at[side, t, x],
+            send_sem=s_send,
+            recv_sem=s_recv.at[t, j],
             device_id=peer("south", souths, 1 if side else -1),
             device_id_type=MESH,
         )
@@ -44,8 +43,8 @@
         return pltpu.make_async_remote_copy(
             src_ref=u.at[t, pl.ds(1, Y), X if side else 1],
             dst_ref=u.at[t, pl.ds(1, Y), 0 if side else X + 1],
-            send_sem=e_send.at[side, t],
-            recv_sem=e_recv.at[side, t],
+            send_sem=e_send,
+            recv_sem=e_recv.at[t],
             device_id=peer("east", easts, 1 if side else -1),
             device_id_type=MESH,
         )
@@ -54,8 +53,8 @@
         return pltpu.make_async_remote_copy(
             src_ref=zs.at[t, side, j],
             dst_ref=zr.at[t, side, j],
-            send_sem=z_send.at[side, t, j],
-            recv_sem=z_recv.at[side, t, j],
+            send_sem=z_send,
+            recv_sem=z_recv.at[t, j],
             device_id=peer("down", downs, 1 if side else -1),
             device_id_type=MESH,
         )
@@ -64,8 +63,8 @@
         return pltpu.make_async_remote_copy(
             src_ref=ms.at[j],
             dst_ref=mr.at[d - 1, j],
-            send_sem=m_send.at[d - 1, j],
-            recv_sem=m_recv.at[d - 1, j],
+            send_sem=m_send,
+            recv_sem=m_recv.at[j],
             device_id=peer("down", downs, d),
             device_id_type=MESH,
         )
@@ -73,13 +72,14 @@
     def south_pair(t, j):
         for side in (0, 1):
             for x in (j, X - 1 - j):
-                south(side, t, x).start()
-
-    def save_line(t, y, x):
-        return pltpu.make_async_copy(u.at[t, pl.ds(1, Y), x + 1], tr_o.at[:, x], out_sem.at[0, x])
-
-    def save_std(x):
-        return pltpu.make_async_copy(st.at[:, x], std_o.at[:, x], out_sem.at[1, x])
+                south(side, t, j, x).start()
+
+    def arrived(ref, sem):
+        everything = pltpu.make_async_remote_copy(
+            src_ref=ref, dst_ref=ref, send_sem=sem, recv_sem=sem,
+            device_id=peer("south", souths, 1), device_id_type=MESH,
+        )
+        everything.wait_recv()
 
     loads = [
         pltpu.make_async_copy(tr.at[y], u.at[0, y + 1, pl.ds(1, X)], in_sem.at[y])
@@ -132,15 +132,12 @@
     top, bottom = level == 0, level == Z - 1
 
     def advance(t, j):
-        for side in (0, 1):
-            down(side, t, j).wait_recv()
-            for x in (j, X - 1 - j):
-                south(side, t, x).wait_recv()
+        arrived(zr.at[t, :, j], z_recv.at[t, j])
+        arrived(u.at[t, 0, pl.ds(0, 4)], s_recv.at[t, j])
 
         @pl.when(j == 0)
         def _():
-            for side in (0, 1):
-                east(side, t).wait_recv()
+            arrived(u.at[t, pl.ds(1, Y), pl.ds(0, 2)], e_recv.at[t])
 
         for r, x in enumerate((j, X - 1 - j)):
             for y in range(Y):
@@ -151,19 +148,19 @@
                 spread = u[t, y, x + 1] + u[t, y + 2, x + 1] + u[t, y + 1, x] + u[t, y + 1, x + 2]
                 spread = spread + before + after - 6.0 * middle
                 value = middle + m[y, x] * spread + s[y, x]
-                u[t + 1, y + 1, x + 1] = value
                 if t + 1 < STEPS:
+                    u[t + 1, y + 1, x + 1] = value
                     zs[t + 1, 0, j, at_row, :] = value[:1]
                     zs[t + 1, 1, j, at_row, :] = value[Z - 1 :]
                 else:
+                    end[y, x] = value
                     mean = jnp.sum(value, axis=0, keepdims=True) * (1.0 / Z)
                     off = value - mean
                     ms[j, 0, at_row, :] = mean
                     ms[j, 1, at_row, :] = jnp.sum(off * off, axis=0, keepdims=True)
 
     def finish(j):
-        for d in range(1, downs):
-            moments(d, j).wait_recv()
+        arrived(mr.at[:, j], m_recv.at[j])
         means = [ms[j, 0]] + [mr[d, j, 0] for d in range(downs - 1)]
         total = functools.reduce(jnp.add, means)
         spreads = functools.reduce(jnp.add, [ms[j, 1]] + [mr[d, j, 1] for d in range(downs - 1)])
@@ -174,9 +171,7 @@
         for r, x in enumerate((j, X - 1 - j)):
             for y in range(Y):
                 k = r * Y + y
-                st[y, x] = (u[STEPS, y + 1, x + 1] - mean[k : k + 1]) * scale[k : k + 1]
-        for x in (j, X - 1 - j):
-            save_std(x).start()
+                st[y, x] = (end[y, x] - mean[k : k + 1]) * scale[k : k + 1]
 
     for t in range(STEPS):
 
@@ -196,8 +191,6 @@
             else:
                 for d in range(1, downs):
                     moments(d, j).start()
-                for x in (j, X - 1 - j):
-                    save_line(STEPS, 0, x).start()
 
                 @pl.when(j + AHEAD < pairs)
                 def _():
@@ -217,28 +210,21 @@
 
     lax.fori_loop(pairs - LAG, pairs, tail, 0)
 
-    def drain(x, carry):
-        save_line(STEPS, 0, x).wait()
-        save_std(x).wait()
-        for side in (0, 1):
-            for t in range(STEPS):
-                south(side, t, x).wait_send()
-        return carry
-
-    lax.fori_loop(0, X, drain, 0)
-
-    def drain_pairs(j, carry):
-        for side in (0, 1):
-            for t in range(STEPS):
-                down(side, t, j).wait_send()
-        for d in range(1, downs):
-            moments(d, j).wait_send()
-        return carry
-
-    lax.fori_loop(0, pairs, drain_pairs, 0)
-    for side in (0, 1):
-        for t in range(STEPS):
-            east(side, t).wait_send()
+    arrived(u.at[:, pl.ds(0, 2), pl.ds(1, X)], s_send)
+    arrived(u.at[:, pl.ds(0, 2), pl.ds(0, Y)], e_send)
+    arrived(zs, z_send)
+    arrived(mr, m_send)
+
+
+def put_out(std, end, std_o, end_o, sem):
+    copies = [
+        pltpu.make_async_copy(std, std_o, sem.at[0]),
+        pltpu.make_async_copy(end, end_o, sem.at[1]),
+    ]
+    for copy in copies:
+        copy.start()
+    for copy in copies:
+        copy.wait()
 
 
 def body(tracer, mobility, source):
@@ -247,16 +233,16 @@
     downs, pairs = sizes[2], X // 2
     f32 = jnp.float32
     dma = pltpu.SemaphoreType.DMA
-    shape = jax.ShapeDtypeStruct(tracer.shape, f32)
+    result = pltpu.VMEM(tracer.shape, f32)
     anywhere = pl.BlockSpec(memory_space=pl.ANY)
-    return pl.pallas_call(
+    onchip = pl.BlockSpec(memory_space=pltpu.VMEM)
+    standardized, final = pl.pallas_call(
         functools.partial(kernel, sizes),
-        out_shape=(shape, shape),
+        out_shape=(result, result),
         in_specs=[anywhere] * 3,
-        out_specs=(anywhere, anywhere),
+        out_specs=(onchip, onchip),
         scratch_shapes=[
-            pltpu.VMEM((STEPS + 1, Y + 2, X + 2, Z, L), f32),
-            pltpu.VMEM((Y, X, Z, L), f32),
+            pltpu.VMEM((STEPS, Y + 2, X + 2, Z, L), f32),
             pltpu.VMEM((Y, X, Z, L), f32),
             pltpu.VMEM((Y, X, Z, L), f32),
             pltpu.VMEM((STEPS, 2, pairs, 2 * Y, L), f32),
@@ -264,20 +250,28 @@
             pltpu.VMEM((pairs, 2, 2 * Y, L), f32),
             pltpu.VMEM((downs - 1, pairs, 2, 2 * Y, L), f32),
             dma((Y + 2,)),
-            dma((2, X)),
-            dma((2, STEPS, X)),
-            dma((2, STEPS, X)),
-            dma((2, STEPS)),
-            dma((2, STEPS)),
-            dma((2, STEPS, pairs)),
-            dma((2, STEPS, pairs)),
-            dma((downs - 1, pairs)),
-            dma((downs - 1, pairs)),
+            dma,
+            dma((STEPS, pairs)),
+            dma,
+            dma((STEPS,)),
+            dma,
+            dma((STEPS, pairs)),
+            dma,
+            dma((pairs,)),
         ],
         compiler_params=pltpu.CompilerParams(
-            collective_id=0, has_side_effects=True, vmem_limit_bytes=60 * 1024 * 1024
+            collective_id=0, has_side_effects=True, vmem_limit_bytes=53 * 1024 * 1024
         ),
     )(tracer, mobility, source)
+    shape = jax.ShapeDtypeStruct(tracer.shape, f32)
+    return pl.pallas_call(
+        put_out,
+        out_shape=(shape, shape),
+        in_specs=[onchip] * 2,
+        out_specs=(anywhere, anywhere),
+        scratch_shapes=[dma((2,))],
+        compiler_params=pltpu.CompilerParams(vmem_limit_bytes=1024 * 1024),
+    )(standardized, final)
 
 
 def solution(mesh):

time: 103 us -> 95.3 us (0.925)
  local copies, waits for them, and re-layouts: 6.87 us -> 0 us
    unnamed x4 -> x0, local copies, waits for them, and re-layouts: 6.87 us -> none
    pallas_call x1 -> x2, Pallas kernels: 95 us -> 94.5 us  [the longest x1 91.1 us: body(): pl.pallas_call(functools.partial(kernel, sizes), out_shape=(result, resul...]
where the time goes in v2:
time: 95.3 us; the launch traced here: 95.2 us
  Pallas kernels  94.5 us (99%)
    pallas_call x1, Pallas kernels, body(): pl.pallas_call(functools.partial(kernel, sizes), out_shape=(result, resul...  91.1 us
    pallas_call x1, Pallas kernels, body(): pl.pallas_call(put_out, out_shape=(shape, shape), in_specs=[onchip] * 2,...  3.41 us

profile of v2, /device:TPU:1, one launch (start us, length us, event | category | flops | bytes accessed | tf_op | source)
XLA Modules:
  0.0 95.2 jit_solution(16110447359520343250)
XLA Ops:
  0.6 91.1 %shard_map.50 = (f32[4,16,128,128]{3,2,1,0:T(8,128)S(1)}, f32[4,16,128,128]{3,2,1,0:T(8,128)S(1)}) custom-call(f32[4,16,128,128]{3,2,1,0:T(8,128)} %tr.1, f32[4,16,128,128]{3,2,1,0:T(8,128)} %mo.1, f32[4,16,128,128]{3,2,1,0:T(8,128)} %so.1), custom_call_target="tpu_custom_call" | custom-call | tf_op jit(solution)/shard_map/pallas_call | solution.py:239
  91.8 3.4 %shard_map.51 = (f32[4,16,128,128]{3,2,1,0:T(8,128)}, f32[4,16,128,128]{3,2,1,0:T(8,128)}) custom-call(f32[4,16,128,128]{3,2,1,0:T(8,128)S(1)} %get-tuple-element.4.std, f32[4,16,128,128]{3,2,1,0:T(8,128)S(1)} %get-tuple-element.5.end), custom_call_target="tpu_custom_call" | custom-call | tf_op jit(solution)/shard_map/pallas_call | solution.py:267

commit v3 on v2

--- a/solution.py
+++ b/solution.py
@@ -8,7 +8,8 @@
 from jax.sharding import PartitionSpec as P
 
 STEPS = 3
-AHEAD = 4
+FIRST = 3
+AHEAD = 6
 LAG = 3
 MESH = pl.DeviceIdType.MESH
 
@@ -18,16 +19,25 @@
     tr, mo, so,
     st, end,
     u, m, s, zs, zr, ms, mr,
-    in_sem, s_send, s_recv, e_send, e_recv, z_send, z_recv, m_send, m_recv,
+    known, in_sem, s_send, s_recv, e_send, e_recv, z_send, z_recv, m_send, m_recv,
 ):
-    souths, easts, downs = sizes
+    trials, souths, easts, downs = sizes
     Y, X, Z, L = tr.shape
     pairs = X // 2
     rows = 2 * Y
-    at = {name: lax.axis_index(name) for name in ("south", "east", "down")}
+    at = {name: lax.axis_index(name) for name in ("trial", "south", "east", "down")}
 
     def peer(name, count, shift):
         return {name: lax.rem(at[name] + shift + count, count)}
+
+    def away(dy=0, dz=0):
+        y = lax.rem(at["down"] % 2 * 2 + at["south"] // 2 + dy + 4, 4)
+        z = lax.rem(at["down"] // 2 * trials + at["trial"] + dz + 2 * trials, 2 * trials)
+        return {
+            "trial": z % trials,
+            "south": y % 2 * 2 + at["south"] % 2,
+            "down": z // trials * 2 + y // 2,
+        }
 
     def south(side, t, j, x):
         return pltpu.make_async_remote_copy(
@@ -95,15 +105,21 @@
         copy.start()
 
     barrier = pltpu.get_barrier_semaphore()
-    greet = [peer("south", souths, d) for d in (-1, 1)]
-    greet += [peer("east", easts, d) for d in (-1, 1)]
-    greet += [peer("down", downs, d) for d in range(1, downs)]
-    for who in greet:
+    near = [peer("south", souths, d) for d in (-1, 1)]
+    near += [peer("east", easts, d) for d in (-1, 1)]
+    near += [away(dy=d) for d in (-1, 1)] + [away(dz=d) for d in (-1, 1)]
+    for who in near:
         pl.semaphore_signal(barrier, inc=1, device_id=who, device_id_type=MESH)
-    pl.semaphore_wait(barrier, len(greet))
-
-    for copy in loads:
-        copy.wait()
+    pl.semaphore_wait(barrier, len(near))
+
+    loads[0].wait()
+    loads[Y - 1].wait()
+    for j in range(FIRST):
+        south_pair(0, j)
+    for y in range(1, Y - 1):
+        loads[y].wait()
+    for side in (0, 1):
+        east(side, 0).start()
 
     def first_faces(j, carry):
         for r, x in enumerate((j, X - 1 - j)):
@@ -113,9 +129,12 @@
         return carry
 
     lax.fori_loop(0, pairs, first_faces, 0)
-    south_pair(0, 0)
-    for side in (0, 1):
-        east(side, 0).start()
+
+    rounds = ([away(dz=-1), away(dz=1)], [away(dz=-2)], [away(dy=-1)], [away(dy=-1)])
+    for i, to in enumerate(rounds):
+        for who in to:
+            pl.semaphore_signal(known.at[i], inc=1, device_id=who, device_id_type=MESH)
+        pl.semaphore_wait(known.at[i], len(to))
 
     def first_down(j, carry):
         for side in (0, 1):
@@ -123,7 +142,7 @@
         return carry
 
     lax.fori_loop(0, pairs, first_down, 0)
-    for j in range(1, AHEAD):
+    for j in range(FIRST, AHEAD):
         south_pair(0, j)
     for copy in others:
         copy.wait()
@@ -228,9 +247,9 @@
 
 
 def body(tracer, mobility, source):
-    sizes = tuple(lax.axis_size(a) for a in ("south", "east", "down"))
+    sizes = tuple(lax.axis_size(a) for a in ("trial", "south", "east", "down"))
     Y, X, Z, L = tracer.shape
-    downs, pairs = sizes[2], X // 2
+    downs, pairs = sizes[3], X // 2
     f32 = jnp.float32
     dma = pltpu.SemaphoreType.DMA
     result = pltpu.VMEM(tracer.shape, f32)
@@ -249,6 +268,7 @@
             pltpu.VMEM((STEPS, 2, pairs, 2 * Y, L), f32),
             pltpu.VMEM((pairs, 2, 2 * Y, L), f32),
             pltpu.VMEM((downs - 1, pairs, 2, 2 * Y, L), f32),
+            pltpu.SemaphoreType.REGULAR((4,)),
             dma((Y + 2,)),
             dma,
             dma((STEPS, pairs)),

time: 95.3 us -> 95.1 us (level)
  no operation moved by 1% of the time
where the time goes in v3:
time: 95.1 us; the launch traced here: 95 us
  Pallas kernels  94.4 us (99%)
    pallas_call x1, Pallas kernels, body(): pl.pallas_call(functools.partial(kernel, sizes), out_shape=(result, resul...  91 us
    pallas_call x1, Pallas kernels, body(): pl.pallas_call(put_out, out_shape=(shape, shape), in_specs=[onchip] * 2,...  3.41 us

profile of v3, /device:TPU:1, one launch (start us, length us, event | category | flops | bytes accessed | tf_op | source)
XLA Modules:
  0.0 95.0 jit_solution(17742161493374577102)
XLA Ops:
  0.6 91.0 %shard_map.50 = (f32[4,16,128,128]{3,2,1,0:T(8,128)S(1)}, f32[4,16,128,128]{3,2,1,0:T(8,128)S(1)}) custom-call(f32[4,16,128,128]{3,2,1,0:T(8,128)} %tr.1, f32[4,16,128,128]{3,2,1,0:T(8,128)} %mo.1, f32[4,16,128,128]{3,2,1,0:T(8,128)} %so.1), custom_call_target="tpu_custom_call" | custom-call | tf_op jit(solution)/shard_map/pallas_call | solution.py:258
  91.6 3.4 %shard_map.51 = (f32[4,16,128,128]{3,2,1,0:T(8,128)}, f32[4,16,128,128]{3,2,1,0:T(8,128)}) custom-call(f32[4,16,128,128]{3,2,1,0:T(8,128)S(1)} %get-tuple-element.4.std, f32[4,16,128,128]{3,2,1,0:T(8,128)S(1)} %get-tuple-element.5.end), custom_call_target="tpu_custom_call" | custom-call | tf_op jit(solution)/shard_map/pallas_call | solution.py:287

commit v4 on v3

--- a/solution.py
+++ b/solution.py
@@ -10,7 +10,7 @@
 STEPS = 3
 FIRST = 3
 AHEAD = 6
-LAG = 3
+DIRECT = 2
 MESH = pl.DeviceIdType.MESH
 
 
@@ -18,7 +18,7 @@
     sizes,
     tr, mo, so,
     st, end,
-    u, m, s, zs, zr, ms, mr,
+    u, m, s, zs, zr, ms, mz, mc, my, mr,
     known, in_sem, s_send, s_recv, e_send, e_recv, z_send, z_recv, m_send, m_recv,
 ):
     trials, souths, easts, downs = sizes
@@ -26,6 +26,9 @@
     pairs = X // 2
     rows = 2 * Y
     at = {name: lax.axis_index(name) for name in ("trial", "south", "east", "down")}
+
+    across = 2
+    beside = 1 + at["down"] % 2 * 2
 
     def peer(name, count, shift):
         return {name: lax.rem(at[name] + shift + count, count)}
@@ -69,12 +72,14 @@
             device_id_type=MESH,
         )
 
-    def moments(d, j):
+    merged = pairs - DIRECT
+
+    def share(src, dst, d, i):
         return pltpu.make_async_remote_copy(
-            src_ref=ms.at[j],
-            dst_ref=mr.at[d - 1, j],
-            send_sem=m_send,
-            recv_sem=m_recv.at[j],
+            src_ref=src,
+            dst_ref=dst,
+            send_sem=m_send.at[i],
+            recv_sem=m_recv.at[i],
             device_id=peer("down", downs, d),
             device_id_type=MESH,
         )
@@ -178,15 +183,8 @@
                     ms[j, 0, at_row, :] = mean
                     ms[j, 1, at_row, :] = jnp.sum(off * off, axis=0, keepdims=True)
 
-    def finish(j):
-        arrived(mr.at[:, j], m_recv.at[j])
-        means = [ms[j, 0]] + [mr[d, j, 0] for d in range(downs - 1)]
-        total = functools.reduce(jnp.add, means)
-        spreads = functools.reduce(jnp.add, [ms[j, 1]] + [mr[d, j, 1] for d in range(downs - 1)])
-        mean = total * (1.0 / downs)
-        between = functools.reduce(jnp.add, [(a - mean) * (a - mean) for a in means])
-        variance = (spreads + between * Z) * (1.0 / (Z * downs))
-        scale = lax.rsqrt(variance + 0.0001)
+    def finish(j, mean, spreads):
+        scale = lax.rsqrt(spreads * (1.0 / (Z * downs)) + 0.0001)
         for r, x in enumerate((j, X - 1 - j)):
             for y in range(Y):
                 k = r * Y + y
@@ -208,38 +206,68 @@
                 n = t * pairs + j + AHEAD
                 south_pair(n // pairs, n % pairs)
             else:
-                for d in range(1, downs):
-                    moments(d, j).start()
+
+                @pl.when(j < merged)
+                def _():
+                    share(ms.at[j], mz.at[j], across, 0).start()
+
+                @pl.when(j >= merged)
+                def _():
+                    k = j - merged
+                    for d in range(1, downs):
+                        share(ms.at[j], mr.at[k, d - 1], d, 2 + k).start()
 
                 @pl.when(j + AHEAD < pairs)
                 def _():
                     south_pair(t, j + AHEAD)
 
-                @pl.when(j >= LAG)
-                def _():
-                    finish(j - LAG)
-
             return carry
 
         lax.fori_loop(0, pairs, step, 0)
 
-    def tail(j, carry):
-        finish(j)
-        return carry
-
-    lax.fori_loop(pairs - LAG, pairs, tail, 0)
+    arrived(mz, m_recv.at[0])
+
+    def merge(j, carry):
+        gap = ms[j, 0] - mz[j, 0]
+        mc[j, 0] = (ms[j, 0] + mz[j, 0]) * 0.5
+        mc[j, 1] = ms[j, 1] + mz[j, 1] + gap * gap * (0.5 * Z)
+        return carry
+
+    lax.fori_loop(0, merged, merge, 0)
+    share(mc, my, beside, 1).start()
+    arrived(my, m_recv.at[1])
+
+    def finish_merged(j, carry):
+        gap = mc[j, 0] - my[j, 0]
+        finish(j, (mc[j, 0] + my[j, 0]) * 0.5, mc[j, 1] + my[j, 1] + gap * gap * (1.0 * Z))
+        return carry
+
+    lax.fori_loop(0, merged, finish_merged, 0)
+
+    def finish_direct(k, carry):
+        j = merged + k
+        arrived(mr.at[k], m_recv.at[2 + k])
+        means = [ms[j, 0]] + [mr[k, d, 0] for d in range(downs - 1)]
+        mean = functools.reduce(jnp.add, means) * (1.0 / downs)
+        spreads = functools.reduce(jnp.add, [ms[j, 1]] + [mr[k, d, 1] for d in range(downs - 1)])
+        between = functools.reduce(jnp.add, [(a - mean) * (a - mean) for a in means])
+        finish(j, mean, spreads + between * Z)
+        return carry
+
+    lax.fori_loop(0, DIRECT, finish_direct, 0)
 
     arrived(u.at[:, pl.ds(0, 2), pl.ds(1, X)], s_send)
     arrived(u.at[:, pl.ds(0, 2), pl.ds(0, Y)], e_send)
     arrived(zs, z_send)
-    arrived(mr, m_send)
+    for i, ref in enumerate([mz, my] + [mr.at[k] for k in range(DIRECT)]):
+        arrived(ref, m_send.at[i])
 
 
 def put_out(std, end, std_o, end_o, sem):
-    copies = [
-        pltpu.make_async_copy(std, std_o, sem.at[0]),
-        pltpu.make_async_copy(end, end_o, sem.at[1]),
-    ]
+    copies = []
+    for y in range(std.shape[0]):
+        copies.append(pltpu.make_async_copy(end.at[y], end_o.at[y], sem.at[0, y]))
+        copies.append(pltpu.make_async_copy(std.at[y], std_o.at[y], sem.at[1, y]))
     for copy in copies:
         copy.start()
     for copy in copies:
@@ -267,7 +295,10 @@
             pltpu.VMEM((STEPS, 2, pairs, 2 * Y, L), f32),
             pltpu.VMEM((STEPS, 2, pairs, 2 * Y, L), f32),
             pltpu.VMEM((pairs, 2, 2 * Y, L), f32),
-            pltpu.VMEM((downs - 1, pairs, 2, 2 * Y, L), f32),
+            pltpu.VMEM((pairs - DIRECT, 2, 2 * Y, L), f32),
+            pltpu.VMEM((pairs - DIRECT, 2, 2 * Y, L), f32),
+            pltpu.VMEM((pairs - DIRECT, 2, 2 * Y, L), f32),
+            pltpu.VMEM((DIRECT, downs - 1, 2, 2 * Y, L), f32),
             pltpu.SemaphoreType.REGULAR((4,)),
             dma((Y + 2,)),
             dma,
@@ -276,8 +307,8 @@
             dma((STEPS,)),
             dma,
             dma((STEPS, pairs)),
-            dma,
-            dma((pairs,)),
+            dma((2 + DIRECT,)),
+            dma((2 + DIRECT,)),
         ],
         compiler_params=pltpu.CompilerParams(
             collective_id=0, has_side_effects=True, vmem_limit_bytes=53 * 1024 * 1024
@@ -289,7 +320,7 @@
         out_shape=(shape, shape),
         in_specs=[onchip] * 2,
         out_specs=(anywhere, anywhere),
-        scratch_shapes=[dma((2,))],
+        scratch_shapes=[dma((2, Y))],
         compiler_params=pltpu.CompilerParams(vmem_limit_bytes=1024 * 1024),
     )(standardized, final)
 

time: 95.1 us -> 93.2 us (0.980)
  Pallas kernels: 94.4 us -> 92.5 us
    pallas_call x1, Pallas kernels: 91 us -> 89.1 us  [body(): pl.pallas_call(functools.partial(kernel, sizes), out_shape=(result, resul...]
where the time goes in v4:
time: 93.2 us; the launch traced here: 93.1 us
  Pallas kernels  92.5 us (99%)
    pallas_call x1, Pallas kernels, body(): pl.pallas_call(functools.partial(kernel, sizes), out_shape=(result, resul...  89.1 us
    pallas_call x1, Pallas kernels, body(): pl.pallas_call(put_out, out_shape=(shape, shape), in_specs=[onchip] * 2,...  3.37 us

profile of v4, /device:TPU:1, one launch (start us, length us, event | category | flops | bytes accessed | tf_op | source)
XLA Modules:
  0.0 93.1 jit_solution(14115688213089651475)
XLA Ops:
  0.6 89.1 %shard_map.50 = (f32[4,16,128,128]{3,2,1,0:T(8,128)S(1)}, f32[4,16,128,128]{3,2,1,0:T(8,128)S(1)}) custom-call(f32[4,16,128,128]{3,2,1,0:T(8,128)} %tr.1, f32[4,16,128,128]{3,2,1,0:T(8,128)} %mo.1, f32[4,16,128,128]{3,2,1,0:T(8,128)} %so.1), custom_call_target="tpu_custom_call" | custom-call | tf_op jit(solution)/shard_map/pallas_call | solution.py:286
  89.7 3.4 %shard_map.51 = (f32[4,16,128,128]{3,2,1,0:T(8,128)}, f32[4,16,128,128]{3,2,1,0:T(8,128)}) custom-call(f32[4,16,128,128]{3,2,1,0:T(8,128)S(1)} %get-tuple-element.4.std, f32[4,16,128,128]{3,2,1,0:T(8,128)S(1)} %get-tuple-element.5.end), custom_call_target="tpu_custom_call" | custom-call | tf_op jit(solution)/shard_map/pallas_call | solution.py:318

commit v5 on v4

--- a/solution.py
+++ b/solution.py
@@ -9,7 +9,8 @@
 
 STEPS = 3
 FIRST = 3
-AHEAD = 6
+AHEAD = 4
+RELAY = 4
 DIRECT = 2
 MESH = pl.DeviceIdType.MESH
 
@@ -18,8 +19,8 @@
     sizes,
     tr, mo, so,
     st, end,
-    u, m, s, zs, zr, ms, mz, mc, my, mr,
-    known, in_sem, s_send, s_recv, e_send, e_recv, z_send, z_recv, m_send, m_recv,
+    u, m, s, zs, zr, rl, ms, mz, mc, my, mr,
+    known, in_sem, s_send, s_recv, e_send, e_recv, z_send, z_recv, r_send, r_recv, m_send, m_recv,
 ):
     trials, souths, easts, downs = sizes
     Y, X, Z, L = tr.shape
@@ -68,9 +69,45 @@
             dst_ref=zr.at[t, side, j],
             send_sem=z_send,
             recv_sem=z_recv.at[t, j],
-            device_id=peer("down", downs, 1 if side else -1),
-            device_id_type=MESH,
-        )
+            device_id=peer("down", downs, 2 * side - 1),
+            device_id_type=MESH,
+        )
+
+    early = at["down"] // 2 == 0
+    inner = 1 - at["down"] % 2
+
+    def hand(t, j):
+        return pltpu.make_async_remote_copy(
+            src_ref=zs.at[t, 1 - inner, j],
+            dst_ref=rl.at[t - 1, j],
+            send_sem=z_send,
+            recv_sem=r_recv.at[t - 1, j],
+            device_id=peer("down", downs, beside),
+            device_id_type=MESH,
+        )
+
+    def forward(t, j):
+        arrived(rl.at[t - 1, j], r_recv.at[t - 1, j])
+        onward = pltpu.make_async_remote_copy(
+            src_ref=rl.at[t - 1, j],
+            dst_ref=zr.at[t, inner, j],
+            send_sem=r_send,
+            recv_sem=z_recv.at[t, j],
+            device_id=peer("down", downs, across),
+            device_id_type=MESH,
+        )
+        onward.start()
+
+    def faces(t, j):
+        @pl.when(early)
+        def _():
+            down(inner, t, j).start()
+            hand(t, j).start()
+
+        @pl.when(jnp.logical_not(early))
+        def _():
+            for side in (0, 1):
+                down(side, t, j).start()
 
     merged = pairs - DIRECT
 
@@ -193,10 +230,15 @@
     for t in range(STEPS):
 
         def step(j, carry, t=t):
+            n = t * pairs + j - RELAY
+
+            @pl.when(jnp.logical_and(early, jnp.logical_and(n >= 0, n < (STEPS - 1) * pairs)))
+            def _():
+                forward(n // pairs + 1, n % pairs)
+
             advance(t, j)
             if t + 1 < STEPS:
-                for side in (0, 1):
-                    down(side, t + 1, j).start()
+                faces(t + 1, j)
 
                 @pl.when(j == 0)
                 def _():
@@ -259,6 +301,11 @@
     arrived(u.at[:, pl.ds(0, 2), pl.ds(1, X)], s_send)
     arrived(u.at[:, pl.ds(0, 2), pl.ds(0, Y)], e_send)
     arrived(zs, z_send)
+
+    @pl.when(early)
+    def _():
+        arrived(rl, r_send)
+
     for i, ref in enumerate([mz, my] + [mr.at[k] for k in range(DIRECT)]):
         arrived(ref, m_send.at[i])
 
@@ -294,6 +341,7 @@
             pltpu.VMEM((Y, X, Z, L), f32),
             pltpu.VMEM((STEPS, 2, pairs, 2 * Y, L), f32),
             pltpu.VMEM((STEPS, 2, pairs, 2 * Y, L), f32),
+            pltpu.VMEM((STEPS - 1, pairs, 2 * Y, L), f32),
             pltpu.VMEM((pairs, 2, 2 * Y, L), f32),
             pltpu.VMEM((pairs - DIRECT, 2, 2 * Y, L), f32),
             pltpu.VMEM((pairs - DIRECT, 2, 2 * Y, L), f32),
@@ -307,6 +355,8 @@
             dma((STEPS,)),
             dma,
             dma((STEPS, pairs)),
+            dma,
+            dma((STEPS - 1, pairs)),
             dma((2 + DIRECT,)),
             dma((2 + DIRECT,)),
         ],

time: 93.2 us -> 92.6 us (level)
  no operation moved by 1% of the time
where the time goes in v5:
time: 92.6 us; the launch traced here: 92.5 us
  Pallas kernels  91.9 us (99%)
    pallas_call x1, Pallas kernels, body(): pl.pallas_call(functools.partial(kernel, sizes), out_shape=(result, resul...  88.5 us
    pallas_call x1, Pallas kernels, body(): pl.pallas_call(put_out, out_shape=(shape, shape), in_specs=[onchip] * 2,...  3.37 us

profile of v5, /device:TPU:1, one launch (start us, length us, event | category | flops | bytes accessed | tf_op | source)
XLA Modules:
  0.0 92.5 jit_solution(7454593391321695499)
XLA Ops:
  0.6 88.5 %shard_map.50 = (f32[4,16,128,128]{3,2,1,0:T(8,128)S(1)}, f32[4,16,128,128]{3,2,1,0:T(8,128)S(1)}) custom-call(f32[4,16,128,128]{3,2,1,0:T(8,128)} %tr.1, f32[4,16,128,128]{3,2,1,0:T(8,128)} %mo.1, f32[4,16,128,128]{3,2,1,0:T(8,128)} %so.1), custom_call_target="tpu_custom_call" | custom-call | tf_op jit(solution)/shard_map/pallas_call | solution.py:333
  89.1 3.4 %shard_map.51 = (f32[4,16,128,128]{3,2,1,0:T(8,128)}, f32[4,16,128,128]{3,2,1,0:T(8,128)}) custom-call(f32[4,16,128,128]{3,2,1,0:T(8,128)S(1)} %get-tuple-element.4.std, f32[4,16,128,128]{3,2,1,0:T(8,128)S(1)} %get-tuple-element.5.end), custom_call_target="tpu_custom_call" | custom-call | tf_op jit(solution)/shard_map/pallas_call | solution.py:368

commit v6 on v5

--- a/solution.py
+++ b/solution.py
@@ -8,9 +8,9 @@
 from jax.sharding import PartitionSpec as P
 
 STEPS = 3
-FIRST = 3
-AHEAD = 4
-RELAY = 4
+FIRST = 4
+AHEAD = 6
+RELAY = 6
 DIRECT = 2
 MESH = pl.DeviceIdType.MESH
 
@@ -76,21 +76,21 @@
     early = at["down"] // 2 == 0
     inner = 1 - at["down"] % 2
 
-    def hand(t, j):
+    def hand(side, shift, t, j):
         return pltpu.make_async_remote_copy(
-            src_ref=zs.at[t, 1 - inner, j],
-            dst_ref=rl.at[t - 1, j],
+            src_ref=zs.at[t, side, j],
+            dst_ref=rl.at[t - 1, side, j],
             send_sem=z_send,
             recv_sem=r_recv.at[t - 1, j],
-            device_id=peer("down", downs, beside),
+            device_id=peer("down", downs, shift),
             device_id_type=MESH,
         )
 
     def forward(t, j):
-        arrived(rl.at[t - 1, j], r_recv.at[t - 1, j])
+        arrived(rl.at[t - 1, :, j], r_recv.at[t - 1, j])
         onward = pltpu.make_async_remote_copy(
-            src_ref=rl.at[t - 1, j],
-            dst_ref=zr.at[t, inner, j],
+            src_ref=rl.at[t - 1, :, j],
+            dst_ref=zr.at[t, :, j],
             send_sem=r_send,
             recv_sem=z_recv.at[t, j],
             device_id=peer("down", downs, across),
@@ -102,12 +102,12 @@
         @pl.when(early)
         def _():
             down(inner, t, j).start()
-            hand(t, j).start()
+            hand(1 - inner, beside, t, j).start()
 
         @pl.when(jnp.logical_not(early))
         def _():
-            for side in (0, 1):
-                down(side, t, j).start()
+            down(1 - inner, t, j).start()
+            hand(inner, 1 - 2 * inner, t, j).start()
 
     merged = pairs - DIRECT
 
@@ -146,13 +146,30 @@
     for copy in others:
         copy.start()
 
+    y_lo, y_hi = at["south"] // 2, at["down"] % 2
+    z = at["down"] // 2 * trials + at["trial"]
+    turn = 2 * trials - 2
+    answers_below = jnp.logical_and(z >= 1, z <= turn)
+    answers_above = z >= turn
+    greeted = [
+        (answers_below, away(dz=-1)),
+        (answers_above, away(dz=1)),
+        (y_hi == 1, away(dy=2 * y_lo - 1)),
+    ]
     barrier = pltpu.get_barrier_semaphore()
     near = [peer("south", souths, d) for d in (-1, 1)]
     near += [peer("east", easts, d) for d in (-1, 1)]
-    near += [away(dy=d) for d in (-1, 1)] + [away(dz=d) for d in (-1, 1)]
+    near += [away(dy=1 - 2 * y_lo)]
     for who in near:
         pl.semaphore_signal(barrier, inc=1, device_id=who, device_id_type=MESH)
-    pl.semaphore_wait(barrier, len(near))
+    for answers, who in greeted:
+
+        @pl.when(jnp.logical_not(answers))
+        def _(who=who):
+            pl.semaphore_signal(barrier, inc=1, device_id=who, device_id_type=MESH)
+
+    below = (z + 2 * trials - 1) // (2 * trials) - z // (turn + 1)
+    pl.semaphore_wait(barrier, len(near) + below + z // turn + y_hi)
 
     loads[0].wait()
     loads[Y - 1].wait()
@@ -171,6 +188,18 @@
         return carry
 
     lax.fori_loop(0, pairs, first_faces, 0)
+
+    for answers, who in greeted:
+
+        @pl.when(answers)
+        def _(who=who):
+            pl.semaphore_signal(known.at[4], inc=1, device_id=who, device_id_type=MESH)
+
+    answers_due = 3 - below - z // turn - y_hi
+
+    @pl.when(answers_due > 0)
+    def _():
+        pl.semaphore_wait(known.at[4], answers_due)
 
     rounds = ([away(dz=-1), away(dz=1)], [away(dz=-2)], [away(dy=-1)], [away(dy=-1)])
     for i, to in enumerate(rounds):
@@ -341,13 +370,13 @@
             pltpu.VMEM((Y, X, Z, L), f32),
             pltpu.VMEM((STEPS, 2, pairs, 2 * Y, L), f32),
             pltpu.VMEM((STEPS, 2, pairs, 2 * Y, L), f32),
-            pltpu.VMEM((STEPS - 1, pairs, 2 * Y, L), f32),
+            pltpu.VMEM((STEPS - 1, 2, pairs, 2 * Y, L), f32),
             pltpu.VMEM((pairs, 2, 2 * Y, L), f32),
             pltpu.VMEM((pairs - DIRECT, 2, 2 * Y, L), f32),
             pltpu.VMEM((pairs - DIRECT, 2, 2 * Y, L), f32),
             pltpu.VMEM((pairs - DIRECT, 2, 2 * Y, L), f32),
             pltpu.VMEM((DIRECT, downs - 1, 2, 2 * Y, L), f32),
-            pltpu.SemaphoreType.REGULAR((4,)),
+            pltpu.SemaphoreType.REGULAR((5,)),
             dma((Y + 2,)),
             dma,
             dma((STEPS, pairs)),

time: 92.6 us -> 90.8 us (0.981)
  Pallas kernels: 91.9 us -> 90.1 us
    pallas_call x1, Pallas kernels: 88.5 us -> 86.7 us  [body(): pl.pallas_call(functools.partial(kernel, sizes), out_shape=(result, resul...]
where the time goes in v6:
time: 90.8 us; the launch traced here: 90.7 us
  Pallas kernels  90.1 us (99%)
    pallas_call x1, Pallas kernels, body(): pl.pallas_call(functools.partial(kernel, sizes), out_shape=(result, resul...  86.7 us
    pallas_call x1, Pallas kernels, body(): pl.pallas_call(put_out, out_shape=(shape, shape), in_specs=[onchip] * 2,...  3.37 us

profile of v6, /device:TPU:1, one launch (start us, length us, event | category | flops | bytes accessed | tf_op | source)
XLA Modules:
  0.0 90.7 jit_solution(12974767293325865655)
XLA Ops:
  0.6 86.7 %shard_map.50 = (f32[4,16,128,128]{3,2,1,0:T(8,128)S(1)}, f32[4,16,128,128]{3,2,1,0:T(8,128)S(1)}) custom-call(f32[4,16,128,128]{3,2,1,0:T(8,128)} %tr.1, f32[4,16,128,128]{3,2,1,0:T(8,128)} %mo.1, f32[4,16,128,128]{3,2,1,0:T(8,128)} %so.1), custom_call_target="tpu_custom_call" | custom-call | tf_op jit(solution)/shard_map/pallas_call | solution.py:362
  87.4 3.4 %shard_map.51 = (f32[4,16,128,128]{3,2,1,0:T(8,128)}, f32[4,16,128,128]{3,2,1,0:T(8,128)}) custom-call(f32[4,16,128,128]{3,2,1,0:T(8,128)S(1)} %get-tuple-element.4.std, f32[4,16,128,128]{3,2,1,0:T(8,128)S(1)} %get-tuple-element.5.end), custom_call_target="tpu_custom_call" | custom-call | tf_op jit(solution)/shard_map/pallas_call | solution.py:397

commit v7 on v6

--- a/solution.py
+++ b/solution.py
@@ -133,10 +133,16 @@
         )
         everything.wait_recv()
 
-    loads = [
-        pltpu.make_async_copy(tr.at[y], u.at[0, y + 1, pl.ds(1, X)], in_sem.at[y])
-        for y in range(Y)
-    ]
+    def load(y, x, count, i):
+        return pltpu.make_async_copy(
+            tr.at[y, pl.ds(x, count)], u.at[0, y + 1, pl.ds(x + 1, count)], in_sem.at[i]
+        )
+
+    sent = (0, Y - 1)
+    first = [load(y, x, 1, Y + 2 + 2 * a + b) for a, y in enumerate(sent) for b, x in enumerate((0, X - 1))]
+    for copy in first:
+        copy.start()
+    loads = [load(y, 1, X - 2, y) if y in sent else load(y, 0, X, y) for y in range(Y)]
     for y in [0, Y - 1] + list(range(1, Y - 1)):
         loads[y].start()
     others = [
@@ -171,9 +177,12 @@
     below = (z + 2 * trials - 1) // (2 * trials) - z // (turn + 1)
     pl.semaphore_wait(barrier, len(near) + below + z // turn + y_hi)
 
+    for copy in first:
+        copy.wait()
+    south_pair(0, 0)
     loads[0].wait()
     loads[Y - 1].wait()
-    for j in range(FIRST):
+    for j in range(1, FIRST):
         south_pair(0, j)
     for y in range(1, Y - 1):
         loads[y].wait()
@@ -377,7 +386,7 @@
             pltpu.VMEM((pairs - DIRECT, 2, 2 * Y, L), f32),
             pltpu.VMEM((DIRECT, downs - 1, 2, 2 * Y, L), f32),
             pltpu.SemaphoreType.REGULAR((5,)),
-            dma((Y + 2,)),
+            dma((Y + 6,)),
             dma,
             dma((STEPS, pairs)),
             dma,

time: 90.8 us -> 90.9 us (level)
  no operation moved by 1% of the time
where the time goes in v7:
time: 90.9 us; the launch traced here: 90.8 us
  Pallas kernels  90.1 us (99%)
    pallas_call x1, Pallas kernels, body(): pl.pallas_call(functools.partial(kernel, sizes), out_shape=(result, resul...  86.8 us
    pallas_call x1, Pallas kernels, body(): pl.pallas_call(put_out, out_shape=(shape, shape), in_specs=[onchip] * 2,...  3.37 us

profile of v7, /device:TPU:1, one launch (start us, length us, event | category | flops | bytes accessed | tf_op | source)
XLA Modules:
  0.0 90.8 jit_solution(2356480371870077840)
XLA Ops:
  0.6 86.8 %shard_map.50 = (f32[4,16,128,128]{3,2,1,0:T(8,128)S(1)}, f32[4,16,128,128]{3,2,1,0:T(8,128)S(1)}) custom-call(f32[4,16,128,128]{3,2,1,0:T(8,128)} %tr.1, f32[4,16,128,128]{3,2,1,0:T(8,128)} %mo.1, f32[4,16,128,128]{3,2,1,0:T(8,128)} %so.1), custom_call_target="tpu_custom_call" | custom-call | tf_op jit(solution)/shard_map/pallas_call | solution.py:371
  87.4 3.4 %shard_map.51 = (f32[4,16,128,128]{3,2,1,0:T(8,128)}, f32[4,16,128,128]{3,2,1,0:T(8,128)}) custom-call(f32[4,16,128,128]{3,2,1,0:T(8,128)S(1)} %get-tuple-element.4.std, f32[4,16,128,128]{3,2,1,0:T(8,128)S(1)} %get-tuple-element.5.end), custom_call_target="tpu_custom_call" | custom-call | tf_op jit(solution)/shard_map/pallas_call | solution.py:406
